TPU v7x, 32 devices: a whole 2x2x4 slice. The times are simulated.
32 devices in a mesh: grp: 2 (over y), seq: 16 (over z, x, core), head: 1.
Axes of the slice: x: 2, y: 2, z: 4, core: 2. Of those that a mesh axis runs over, the one named last changes fastest.
Arguments:
- queries: bfloat16 [2048, 1, 128], P(('grp', 'seq'), 'head'), parts along dimension 0, may hold values from -6 to 6
- keys: bfloat16 [256, 512, 8, 128], P(('grp', 'seq'), None, 'head'), parts along dimension 0, may hold values from -28 to 28
- values: bfloat16 [256, 512, 8, 128], P(('grp', 'seq'), None, 'head'), parts along dimension 0, may hold values from -6 to 6
- lengths: int32 [32], P('grp'), parts along dimension 0, may hold values from 1 to 4096, 40960 in all
- slot_block: int32 [256], P(('grp', 'seq')), parts along dimension 0, may hold values from 0 to 127, each once
Outputs:
- attended: bfloat16 [2048, 1, 128], P(('grp', 'seq'), 'head'), parts along dimension 0
There are 2 independent parts, one for each index of `grp`. A program takes and returns all parts, laid end to end along the dimension named above; each array names one. Nothing has to cross between parts.
Inputs may be any that keep to these rules, and one draw needn't show every extreme that they name: `slot_block`: each slot holds a different logical block; every block of every sequence has a slot. `lengths`: every sequence has at least one token.
All inputs are finite; a program needn't handle non-finite values.
Results may differ from a plain program's by a relative error of at most 0.0055.
Values may be sent and summed in bfloat16 or wider, within the bound.
A program may use at most 64 MiB of HBM per device.

v0:
```python
import jax
import jax.numpy as jnp
from jax import lax
from jax.sharding import PartitionSpec as P


def slot_partial(q_one, key_one, val_one, live_one, factor):
    scores = jnp.einsum("kgd,tkd->kgt", q_one, key_one, preferred_element_type=jnp.float32) * factor
    live_row = live_one[None, None, :]
    peak = jnp.max(jnp.where(live_row, scores, -1e30), axis=-1)
    weights = jnp.where(live_row, jnp.exp(scores - peak[..., None]), 0.0).astype(jnp.bfloat16)
    total = jnp.sum(weights.astype(jnp.float32), axis=-1)
    partial_out = jnp.einsum("kgt,tkd->kgd", weights, val_one, preferred_element_type=jnp.float32)
    return (peak, total, partial_out)


def body(queries, keys, values, lengths, slot_block):
    rows = lax.all_gather(queries, "seq", axis=0, tiled=True)
    slots, block, kv_local, head_dim = keys.shape
    batch = lengths.shape[0]
    group = rows.shape[0] // batch // kv_local
    factor = head_dim ** (-0.5)
    q_grouped = rows.reshape(batch, kv_local, group, head_dim)
    per_seq = slots * lax.axis_size("seq") // batch
    seq_of = slot_block // per_seq
    blk_of = slot_block % per_seq
    q_slot = jnp.take(q_grouped, seq_of, axis=0)
    positions = blk_of[:, None] * block + jnp.arange(block, dtype=jnp.int32)[None, :]
    live = positions < jnp.take(lengths, seq_of)[:, None]

    def run_slot(q_one, key_one, val_one, live_one):
        return slot_partial(q_one, key_one, val_one, live_one, factor)

    peaks, totals, partials = jax.vmap(run_slot)(q_slot, keys, values, live)
    member = seq_of[:, None] == jnp.arange(batch, dtype=jnp.int32)[None, :]
    best = jnp.max(jnp.where(member[:, :, None, None], peaks[:, None], -1e30), axis=0)
    scaled = jnp.exp(peaks - jnp.take(best, seq_of, axis=0))
    onehot = member.astype(jnp.float32)
    denom = jnp.einsum("sb,skg->bkg", onehot, scaled * totals, precision=lax.Precision.HIGHEST)
    numer = jnp.einsum(
        "sb,skgd->bkgd", onehot, scaled[..., None] * partials, precision=lax.Precision.HIGHEST
    )
    row_count = rows.shape[0]
    share = row_count // lax.axis_size("seq")
    top_peak = lax.pmax(best, "seq")
    rescale = jnp.exp(best - top_peak)
    own_total, own_out = (
        lax.psum_scatter(
            (denom * rescale).reshape(row_count), "seq", scatter_dimension=0, tiled=True
        ),
        lax.psum_scatter(
            (numer * rescale[..., None]).reshape(row_count, head_dim),
            "seq",
            scatter_dimension=0,
            tiled=True,
        ),
    )
    result = own_out / own_total[:, None]
    return result.astype(jnp.bfloat16).reshape(share, 1, head_dim)


def solution(mesh):
    placed = (
        P(("grp", "seq"), "head", None),
        P(("grp", "seq"), None, "head", None),
        P(("grp", "seq"), None, "head", None),
        P("grp"),
        P(("grp", "seq")),
    )
    return jax.shard_map(
        body, mesh=mesh, in_specs=placed, out_specs=P(("grp", "seq"), "head", None), check_vma=False
    )
```

profile of v0, /device:TPU:0, one launch (start us, length us, event | category | flops | bytes accessed | tf_op | source)
XLA Modules:
  0.0 166.0 jit_solution(9803594081013029989)
XLA Ops:
  6.5 0.0 copy-start
  6.5 0.0 reduce-scatter.2.cloned.1.call-start
  6.5 0.7 compare_select_fusion
  7.2 0.1 iota_compare_fusion
  7.3 0.0 copy-done
  7.3 0.6 gather_fusion
  8.0 24.1 %all_gather.3 = bf16[1024,1,128]{2,0,1:T(8,128)(2,1)S(1)} all-gather(bf16[64,1,128]{2,0,1:T(8,128)(2,1)} %param.5), channel_id=1, replica_groups=mesh['grp'=2,'seq'=16,'head'=1] {'seq'}, dimensions={0}, use_global_device_ids=true | all-gather | bytes 278528 | tf_op jit(solution)/shard_map/all_gather | solution.py:18
  32.0 0.6 gather_fusion.1
  32.6 0.1 add_compare_fusion
  32.7 5.8 %select_reduce_fusion = (f32[8,8,8]{2,1,0:T(8,128)S(1)}, f32[8,8,8,512]{3,2,1,0:T(8,128)S(1)}) fusion(pred[8,512]{1,0:T(8,128)(4,1)S(1)} %add_compare_fusion, bf16[8,512,8,128]{3,2,1,0:T(8,128)(2,1)} %param.6, bf16[8,8,8,128]{3,2,1,0:T(8,128)(2,1)S(1)} %gather_fusion.1, pred[8]{0:T(512)(128)(4,1)S(1)} %get-tuple-element.8), kind=kOutput, calls=%fused_computation.14 | convolution fusion | flops 67960320 | bytes 9574408 | tf_op jit(solution)/shard_map/vmap(kgd,tkd->kgt)/dot_general | solution.py:8
  38.4 0.0 copy-start.1
  38.4 0.1 select_reduce_fusion.1
  38.6 57.8 %pmax.7 = f32[16,8,8]{0,2,1:T(8,128)S(1)} all-reduce(f32[16,8,8]{0,2,1:T(8,128)S(1)} %select_reduce_fusion.1), channel_id=1, replica_groups=mesh['grp'=2,'seq'=16,'head'=1] {'seq'}, use_global_device_ids=true, to_apply=%region_2.3 | all-reduce | flops 1024 | bytes 8192 | tf_op jit(solution)/shard_map/pmax | solution.py:45
  96.4 0.1 copy.23
  96.6 0.3 convert_reduce_fusion
  96.9 0.6 gather_fusion.2
  97.5 0.1 fusion.23
  97.6 5.0 %fusion.7 = f32[8,8,8,128]{3,2,1,0:T(8,128)S(1)} fusion(bf16[8,512,8,128]{3,2,1,0:T(8,128)(2,1)} %param.7, f32[8,8,8]{2,1,0:T(8,128)S(1)} %get-tuple-element.6, f32[8,8,8,512]{3,2,1,0:T(8,128)S(1)} %get-tuple-element.13, f32[8,8,8]{2,1,0:T(8,128)S(1)} %get-tuple-element.12, pred[8,512]{1,0:T(8,128)(4,1)S(1)} %add_compare_fusion), kind=kOutput, calls=%fused_computation.9 | convolution fusion | flops 67960832 | bytes 9707520 | tf_op jit(solution)/shard_map/vmap(kgt,tkd->kgd)/dot_general | solution.py:13
  102.5 0.6 convolution_multiply_fusion
  103.1 1.0 copy.26
  104.0 0.0 reduce-scatter.2.cloned.1.call-update
  104.1 0.1 copy.27
  104.2 0.2 fusion.10
  104.4 0.1 copy.28
  104.5 0.1 reshape.84
  104.6 0.0 copy-done.1
  104.6 0.6 dynamic-slice
  105.8 29.6 %all-reduce = f32[1024]{0:T(1024)S(1)} all-reduce(f32[1024]{0:T(1024)S(1)} %reshape.84), channel_id=3, replica_groups=mesh['grp'=2,'seq'=16,'head'=1] {'seq'}, use_global_device_ids=true, to_apply=%region_5.6.clone | all-reduce | flops 1024 | bytes 8192
  135.4 0.1 dynamic-slice.1
  135.5 22.2 %reduce-scatter.2.cloned.1.call-done = f32[64,128]{1,0:T(8,128)} async-done(((f32[1024,128]{1,0:T(8,128)}), f32[64,128]{1,0:T(8,128)}) %reduce-scatter.2.cloned.1.call-update) | async-done | bytes 32784 | tf_op jit(solution)/shard_map/reduce_scatter | solution.py:51
  157.7 1.4 fusion.16
  (3 shorter events, 0.0 us)
Async XLA Ops:
  6.5 0.8 copy-start
  6.5 151.2 %reduce-scatter.2.cloned.1.call-start = ((), (), s32[]{:S(2)}) async-start(), calls=%async_computation.1 | async-start | bytes 557056 | tf_op jit(solution)/shard_map/reduce_scatter | solution.py:51
  38.4 66.1 %copy-start.1 = (u32[32]{0:T(128)S(1)}, u32[32]{0:T(128)}, u32[]{:S(2)}) copy-start(u32[32]{0:T(128)} %constant.84) | copy-start | bytes 388
Sparse Core Ops, SparseCore 0:
  104.2 53.4 reduce-scatter.1
where the time goes:
time: 166 us
  blocking collectives  111 us (67%)
  waiting for transfers between devices  22.2 us (13%)
  between operations  14.1 us (8%)
  matrix products  11.5 us (7%)
  local copies, waits for them, and re-layouts  3.73 us (2%)
  other arithmetic  2.89 us (2%)
    pmax x1, blocking collectives, body(): top_peak = lax.pmax(best, 'seq')  57.8 us
    unnamed x1, blocking collectives  29.6 us
    all_gather x1, blocking collectives, body(): rows = lax.all_gather(queries, 'seq', axis=0, tiled=True)  24.1 us
    reduce_scatter x1, waiting for transfers between devices, body(): lax.psum_scatter((numer * rescale[..., None]).reshape(row_count, head_dim...  22.2 us
    dot_general x1, matrix products, slot_partial(): jnp.einsum('kgd,tkd->kgt', q_one, key_one, preferred_element_type=jnp.flo...  5.79 us
    dot_general x1, matrix products, slot_partial(): jnp.einsum('kgt,tkd->kgd', weights, val_one, preferred_element_type=jnp.f...  4.96 us
  transfers between devices with their start and end apart: 1, of which 1 were waited for; matrix products, arithmetic and copies ran while one was open for 1% of the time, Pallas kernels for 0%

commit v1 on v0

v1 whole, which is shorter than its diff:
```python
import functools
import jax
import jax.numpy as jnp
from jax import lax
from jax.experimental import pallas as pl
from jax.experimental.pallas import tpu as pltpu
from jax.sharding import PartitionSpec as P

LANES = 128
MESH_ID = pl.DeviceIdType.MESH
LOW = -1e30


def spread(tile, start, heads):
    group = tile.shape[0]
    return jnp.concatenate(
        [jnp.broadcast_to(tile[:, start + h : start + h + 1], (group, LANES)) for h in range(heads)],
        axis=0,
    )


def fold(tile, step, op):
    shift = LANES // 2
    while shift >= step:
        tile = op(tile, pltpu.roll(tile, shift, 1))
        shift //= 2
    return tile


def unpack(tile, lane):
    turned = pltpu.roll(tile, LANES // 2, 1)
    low = lane < LANES // 2
    return jnp.where(low, tile, turned), jnp.where(low, turned, tile)


def kernel(
    n, batch, block, kv, factor,
    lengths, slot_block, q_ref, k_hbm, v_hbm, out_ref,
    q_all, k_buf, v_buf, parts, peaks, totals,
    acc, stat, acc_in, stat_in, acc2, stat2, acc2_in, stat2_in,
    k_sem, v_sem, own_sem, qs_sem, qr_sem, fs_sem, s1_sem, r1_sem, s2_sem, r2_sem, t2_sem, u2_sem,
):
    slots, cols, hd = k_buf.shape
    share = q_ref.shape[0]
    outer = n // 2
    per = n // batch
    heads = per * share
    group = heads // kv
    held = share // group
    me = lax.axis_index("seq")
    mine, inner = me // 2, me % 2
    partner = me + 1 - 2 * inner

    def k_copy(s):
        return pltpu.make_async_copy(k_hbm.at[s], k_buf.at[s], k_sem.at[s])

    def v_copy(s):
        return pltpu.make_async_copy(v_hbm.at[s], v_buf.at[s], v_sem.at[s])

    for s in range(slots):
        k_copy(s).start()
        v_copy(s).start()
    own = pltpu.make_async_copy(q_ref, q_all.at[me], own_sem)
    own.start()

    peers = [(mine + r) % outer for r in range(1, outer)]
    barrier = pltpu.get_barrier_semaphore()
    pl.semaphore_signal(barrier, inc=1, device_id={"seq": partner}, device_id_type=MESH_ID)
    for o in peers:
        pl.semaphore_signal(barrier, inc=1, device_id={"seq": o * 2 + inner}, device_id_type=MESH_ID)
    pl.semaphore_wait(barrier, outer)

    def remote(src, dst, ssem, rsem, dev):
        return pltpu.make_async_remote_copy(
            src_ref=src, dst_ref=dst, send_sem=ssem, recv_sem=rsem,
            device_id={"seq": dev}, device_id_type=MESH_ID,
        )

    sends = []
    for r, o in enumerate(peers):
        sends.append(remote(q_ref, q_all.at[me], qs_sem.at[r], qr_sem.at[me], o * 2 + inner))
    sends.append(remote(q_ref, q_all.at[me], qs_sem.at[outer - 1], qr_sem.at[me], partner))
    for c in sends:
        c.start()
    forwards = []
    for r in range(1, outer):
        src = ((mine + outer - r) % outer) * 2 + inner
        remote(q_ref, q_all.at[src], qs_sem.at[0], qr_sem.at[src], partner).wait_recv()
        c = remote(q_all.at[src], q_all.at[src], fs_sem.at[r - 1], qr_sem.at[src], partner)
        c.start()
        forwards.append(c)
    remote(q_ref, q_all.at[partner], qs_sem.at[0], qr_sem.at[partner], partner).wait_recv()
    for r in range(1, outer):
        src = ((mine + outer - r) % outer) * 2 + 1 - inner
        remote(q_ref, q_all.at[src], qs_sem.at[0], qr_sem.at[src], partner).wait_recv()
    own.wait()

    lane = lax.broadcasted_iota(jnp.int32, (group, LANES), 1)
    chunk = min(cols, 512)
    wide = lax.broadcasted_iota(jnp.int32, (group, chunk), 1)
    picks = [wide % kv == h for h in range(kv)]

    def one_slot(s, carry):
        code = slot_block[s]
        seq = code // (slots * n // batch)
        blk = code % (slots * n // batch)
        limit = (lengths[seq] - blk * block) * kv
        q = q_all[pl.ds(seq * per, per)]
        if per > 1:
            q = q.astype(jnp.float32).reshape(heads, hd).astype(jnp.bfloat16)
        else:
            q = q.reshape(heads, hd)
        k_copy(s).wait()
        scores = []
        top = jnp.full((group, LANES), LOW, jnp.float32)
        for c in range(0, cols, chunk):
            full = lax.dot_general(
                q, k_buf[s, c : c + chunk, :], (((1,), (1,)), ((), ())),
                preferred_element_type=jnp.float32,
            )
            packed = full[:group]
            for h in range(1, kv):
                packed = jnp.where(picks[h], full[h * group : (h + 1) * group], packed)
            packed = jnp.where(wide < limit - c, packed * factor, LOW)
            scores.append(packed)
            for l in range(0, chunk, LANES):
                top = jnp.maximum(top, packed[:, l : l + LANES])
        top = fold(top, kv, jnp.maximum)
        top_wide = jnp.concatenate([top] * (chunk // LANES), axis=1)
        total = jnp.zeros((group, LANES), jnp.float32)
        part = jnp.zeros((heads, hd), jnp.float32)
        v_copy(s).wait()
        for i, c in enumerate(range(0, cols, chunk)):
            weight = jnp.where(wide < limit - c, jnp.exp(scores[i] - top_wide), 0.0)
            weight = weight.astype(jnp.bfloat16).astype(jnp.float32)
            for l in range(0, chunk, LANES):
                total = total + weight[:, l : l + LANES]
            spread_w = jnp.concatenate(
                [jnp.where(picks[h], weight, 0.0) for h in range(kv)], axis=0
            ).astype(jnp.bfloat16)
            part = part + jnp.dot(
                spread_w, v_buf[s, c : c + chunk, :], preferred_element_type=jnp.float32
            )
        parts[s] = part
        peaks[s] = top
        totals[s] = fold(total, kv, jnp.add)
        return carry

    lax.fori_loop(0, slots, one_slot, 0)

    seqs = [slot_block[s] // (slots * n // batch) for s in range(slots)]
    for s in range(slots):
        best = peaks[s]
        for t in range(slots):
            if t != s:
                best = jnp.maximum(best, jnp.where(seqs[t] == seqs[s], peaks[t], LOW))
        scale = jnp.exp(peaks[s] - best)
        totals[s] = totals[s] * scale
        parts[s] = parts[s] * spread(scale, 0, kv)
    low_half = lane < LANES // 2
    for b in range(batch):
        flags = [jnp.where(seqs[s] == b, 1.0, 0.0) for s in range(slots)]
        best = jnp.full((group, LANES), LOW, jnp.float32)
        total = jnp.zeros((group, LANES), jnp.float32)
        out = jnp.zeros((heads, hd), jnp.float32)
        for s in range(slots):
            best = jnp.maximum(best, jnp.where(seqs[s] == b, peaks[s], LOW))
            total = total + flags[s] * totals[s]
            out = out + flags[s] * parts[s]
        for p in range(per):
            j = b * per + p
            turn = (LANES - p * held) % LANES
            tb, tt = best, total
            if turn:
                tb, tt = pltpu.roll(best, turn, 1), pltpu.roll(total, turn, 1)
            stat[j % 2, j // 2] = jnp.where(low_half, tb, tt)
            acc[j % 2, j // 2] = out[p * share : (p + 1) * share]

    c1 = remote(acc.at[1 - inner], acc_in, s1_sem.at[0], r1_sem.at[0], partner)
    c2 = remote(stat.at[1 - inner], stat_in, s1_sem.at[1], r1_sem.at[1], partner)
    c2.start()
    c1.start()
    c2.wait()
    c1.wait()
    last = []
    for r in range(1, outer + 1):
        o = (mine + r) % outer
        ma, la = unpack(stat[inner, o], lane)
        mb, lb = unpack(stat_in[o], lane)
        best = jnp.maximum(ma, mb)
        sa, sb = jnp.exp(ma - best), jnp.exp(mb - best)
        total = sa * la + sb * lb
        both = acc[inner, o] * spread(sa, 0, held) + acc_in[o] * spread(sb, 0, held)
        if r == outer:
            break
        stat2[o] = jnp.where(low_half, best, total)
        acc2[o] = both.astype(jnp.bfloat16)
        dev = o * 2 + inner
        c1 = remote(acc2.at[o], acc2_in.at[mine], s2_sem.at[r - 1], r2_sem.at[mine], dev)
        c2 = remote(stat2.at[o], stat2_in.at[mine], t2_sem.at[r - 1], u2_sem.at[mine], dev)
        c2.start()
        c1.start()
        last += [c1, c2]
    for r in range(1, outer):
        o = (mine + outer - r) % outer
        remote(stat2.at[o], stat2_in.at[o], t2_sem.at[0], u2_sem.at[o], partner).wait_recv()
        remote(acc2.at[o], acc2_in.at[o], s2_sem.at[0], r2_sem.at[o], partner).wait_recv()
        mb, lb = unpack(stat2_in[o], lane)
        new = jnp.maximum(best, mb)
        sa, sb = jnp.exp(best - new), jnp.exp(mb - new)
        total = sa * total + sb * lb
        both = both * spread(sa, 0, held) + acc2_in[o].astype(jnp.float32) * spread(sb, 0, held)
        best = new
    out_ref[...] = (both / spread(total, 0, held)).astype(jnp.bfloat16)
    for c in sends + forwards + last:
        c.wait_send()


def body(queries, keys, values, lengths, slot_block):
    slots, block, kv, hd = keys.shape
    share = queries.shape[0]
    n = lax.axis_size("seq")
    batch = lengths.shape[0]
    heads = n * share // batch
    group = heads // kv
    outer = n // 2
    cols = block * kv
    f32, bf16 = jnp.float32, jnp.bfloat16
    dma = pltpu.SemaphoreType.DMA
    vmem = pl.BlockSpec(memory_space=pltpu.VMEM)
    smem = pl.BlockSpec(memory_space=pltpu.SMEM)
    hbm = pl.BlockSpec(memory_space=pl.ANY)
    result = pl.pallas_call(
        functools.partial(kernel, n, batch, block, kv, hd ** (-0.5)),
        out_shape=jax.ShapeDtypeStruct((share, hd), bf16),
        in_specs=[smem, smem, vmem, hbm, hbm],
        out_specs=vmem,
        scratch_shapes=[
            pltpu.VMEM((n, share, hd), bf16),
            pltpu.VMEM((slots, cols, hd), bf16),
            pltpu.VMEM((slots, cols, hd), bf16),
            pltpu.VMEM((slots, heads, hd), f32),
            pltpu.VMEM((slots, group, LANES), f32),
            pltpu.VMEM((slots, group, LANES), f32),
            pltpu.VMEM((2, outer, share, hd), f32),
            pltpu.VMEM((2, outer, group, LANES), f32),
            pltpu.VMEM((outer, share, hd), f32),
            pltpu.VMEM((outer, group, LANES), f32),
            pltpu.VMEM((outer, share, hd), bf16),
            pltpu.VMEM((outer, group, LANES), f32),
            pltpu.VMEM((outer, share, hd), bf16),
            pltpu.VMEM((outer, group, LANES), f32),
            dma((slots,)), dma((slots,)), dma,
            dma((outer,)), dma((n,)), dma((outer,)),
            dma((2,)), dma((2,)),
            dma((outer,)), dma((outer,)), dma((outer,)), dma((outer,)),
        ],
        compiler_params=pltpu.CompilerParams(
            collective_id=0, has_side_effects=True, vmem_limit_bytes=48 * 1024 * 1024
        ),
        name="decode",
    )(
        lengths,
        slot_block,
        queries.reshape(share, hd),
        keys.reshape(slots, cols, hd),
        values.reshape(slots, cols, hd),
    )
    return result.reshape(share, 1, hd)


def solution(mesh):
    placed = (
        P(("grp", "seq"), "head", None),
        P(("grp", "seq"), None, "head", None),
        P(("grp", "seq"), None, "head", None),
        P("grp"),
        P(("grp", "seq")),
    )
    return jax.shard_map(
        body, mesh=mesh, in_specs=placed, out_specs=P(("grp", "seq"), "head", None), check_vma=False
    )
```

time: 166 us -> 33.3 us (0.20)
  blocking collectives: 111 us -> 0 us
  Pallas kernels: 0 us -> 30.4 us
  waiting for transfers between devices: 22.2 us -> 0 us
  between operations: 14.1 us -> 0.01 us
  matrix products: 11.5 us -> 0 us
  other arithmetic: 2.89 us -> 0 us
    pmax x1 -> x0, blocking collectives: 57.8 us -> none  [body(): top_peak = lax.pmax(best, 'seq')]
    pallas_call x0 -> x1, Pallas kernels: none -> 30.4 us  [body(): pl.pallas_call(functools.partial(kernel, n, batch, block, kv, hd ** (-0.5...]
    unnamed x1 -> x0, blocking collectives: 29.6 us -> none
    all_gather x1 -> x0, blocking collectives: 24.1 us -> none  [body(): rows = lax.all_gather(queries, 'seq', axis=0, tiled=True)]
    reduce_scatter x1 -> x0, waiting for transfers between devices: 22.2 us -> none  [body(): lax.psum_scatter((numer * rescale[..., None]).reshape(row_count, head_dim...]
    dot_general x3 -> x0, matrix products: 11.3 us -> none  [the longest x1 5.79 us: slot_partial(): jnp.einsum('kgd,tkd->kgt', q_one, key_one, preferred_element_type=jnp.flo...]
    unnamed x6 -> x7, local copies, waits for them, and re-layouts: 0.67 us -> 2.63 us
    gather x3 -> x0, local copies, waits for them, and re-layouts: 1.77 us -> none  [the longest x1 0.64 us: body(): live = positions < jnp.take(lengths, seq_of)[:, None]]
  transfers between devices with their start and end apart: 1 -> 0, of which waited for: 1 -> 0; matrix products, arithmetic and copies ran while one was open for 1% -> 0% of each run, Pallas kernels for 0% -> 0%
where the time goes in v1:
time: 33.3 us; the launch traced here: 33.1 us
  Pallas kernels  30.4 us (91%)
  local copies, waits for them, and re-layouts  2.63 us (8%)
    pallas_call x1, Pallas kernels, body(): pl.pallas_call(functools.partial(kernel, n, batch, block, kv, hd ** (-0.5...  30.4 us
    unnamed x7, local copies, waits for them, and re-layouts  2.63 us

profile of v1, /device:TPU:0, one launch (start us, length us, event | category | flops | bytes accessed | tf_op | source)
XLA Modules:
  0.0 33.1 jit_solution(6513704149188892921)
XLA Ops:
  0.0 0.0 copy-start
  0.0 0.7 %copy-done = bf16[64,1,128]{2,0,1:T(8,128)(2,1)S(1)} copy-done((bf16[64,1,128]{2,0,1:T(8,128)(2,1)S(1)}, bf16[64,1,128]{2,0,1:T(8,128)(2,1)}, u32[]{:S(2)}) %copy-start) | copy-done | bytes 16408
  0.7 0.0 copy-start.1
  0.7 0.7 %copy-done.1 = s32[16]{0:T(128)S(1)} copy-done((s32[16]{0:T(128)S(1)}, s32[16]{0:T(128)}, u32[]{:S(2)}) %copy-start.1) | copy-done | bytes 88
  1.4 0.0 copy-start.2
  1.4 0.7 %copy-done.2 = s32[8]{0:T(128)S(1)} copy-done((s32[8]{0:T(128)S(1)}, s32[8]{0:T(128)}, u32[]{:S(2)}) %copy-start.2) | copy-done | bytes 56
  2.0 30.4 %decode.1 = bf16[64,128]{1,0:T(8,128)(2,1)S(1)} custom-call(s32[16]{0:T(128)S(1)} %copy-done.1, s32[8]{0:T(128)S(1)} %copy-done.2, bf16[64,128]{1,0:T(8,128)(2,1)S(1)} %bitcast.5, bf16[8,4096,128]{2,1,0:T(8,128)(2,1)} %bitcast.6, bf16[8,4096,128]{2,1,0:T(8,128)(2,1)} %bitcast.7), custom_call_target="tpu_custom_call" | custom-call | tf_op jit(solution)/shard_map/decode/pallas_call | solution.py:233
  32.5 0.6 %copy.7 = bf16[64,1,128]{2,0,1:T(8,128)(2,1)} copy(bf16[64,1,128]{2,0,1:T(8,128)(2,1)S(1)} %bitcast.4) | data formatting | bytes 32768
Async XLA Ops:
  0.0 0.7 %copy-start = (bf16[64,1,128]{2,0,1:T(8,128)(2,1)S(1)}, bf16[64,1,128]{2,0,1:T(8,128)(2,1)}, u32[]{:S(2)}) copy-start(bf16[64,1,128]{2,0,1:T(8,128)(2,1)} %param.5) | copy-start | bytes 49156
  0.7 0.7 %copy-start.1 = (s32[16]{0:T(128)S(1)}, s32[16]{0:T(128)}, u32[]{:S(2)}) copy-start(s32[16]{0:T(128)} %lengths.1) | copy-start | bytes 196
  1.4 0.7 %copy-start.2 = (s32[8]{0:T(128)S(1)}, s32[8]{0:T(128)}, u32[]{:S(2)}) copy-start(s32[8]{0:T(128)} %slot_block.1) | copy-start | bytes 100

commit v2 on v1

--- a/solution.py
+++ b/solution.py
@@ -35,10 +35,10 @@
 
 def kernel(
     n, batch, block, kv, factor,
-    lengths, slot_block, q_ref, k_hbm, v_hbm, out_ref,
-    q_all, k_buf, v_buf, parts, peaks, totals,
+    lengths_hbm, block_hbm, q_hbm, k_hbm, v_hbm, out_ref,
+    lengths, slot_block, q_ref, q_all, k_buf, v_buf, parts, peaks, totals,
     acc, stat, acc_in, stat_in, acc2, stat2, acc2_in, stat2_in,
-    k_sem, v_sem, own_sem, qs_sem, qr_sem, fs_sem, s1_sem, r1_sem, s2_sem, r2_sem, t2_sem, u2_sem,
+    k_sem, v_sem, own_sem, in_sem, qs_sem, qr_sem, fs_sem, s1_sem, r1_sem, s2_sem, r2_sem, t2_sem, u2_sem,
 ):
     slots, cols, hd = k_buf.shape
     share = q_ref.shape[0]
@@ -57,17 +57,23 @@
     def v_copy(s):
         return pltpu.make_async_copy(v_hbm.at[s], v_buf.at[s], v_sem.at[s])
 
-    for s in range(slots):
-        k_copy(s).start()
-        v_copy(s).start()
-    own = pltpu.make_async_copy(q_ref, q_all.at[me], own_sem)
-    own.start()
-
+    q_in = pltpu.make_async_copy(q_hbm, q_ref, in_sem.at[0])
+    q_in.start()
     peers = [(mine + r) % outer for r in range(1, outer)]
     barrier = pltpu.get_barrier_semaphore()
     pl.semaphore_signal(barrier, inc=1, device_id={"seq": partner}, device_id_type=MESH_ID)
     for o in peers:
         pl.semaphore_signal(barrier, inc=1, device_id={"seq": o * 2 + inner}, device_id_type=MESH_ID)
+    len_in = pltpu.make_async_copy(lengths_hbm, lengths, in_sem.at[1])
+    block_in = pltpu.make_async_copy(block_hbm, slot_block, in_sem.at[2])
+    len_in.start()
+    block_in.start()
+    own = pltpu.make_async_copy(q_hbm, q_all.at[me], own_sem)
+    own.start()
+    for s in range(slots):
+        k_copy(s).start()
+        v_copy(s).start()
+    q_in.wait()
     pl.semaphore_wait(barrier, outer)
 
     def remote(src, dst, ssem, rsem, dev):
@@ -93,7 +99,12 @@
     for r in range(1, outer):
         src = ((mine + outer - r) % outer) * 2 + 1 - inner
         remote(q_ref, q_all.at[src], qs_sem.at[0], qr_sem.at[src], partner).wait_recv()
+    for s in range(slots):
+        k_copy(s).wait()
+        v_copy(s).wait()
     own.wait()
+    len_in.wait()
+    block_in.wait()
 
     lane = lax.broadcasted_iota(jnp.int32, (group, LANES), 1)
     chunk = min(cols, 512)
@@ -110,7 +121,6 @@
             q = q.astype(jnp.float32).reshape(heads, hd).astype(jnp.bfloat16)
         else:
             q = q.reshape(heads, hd)
-        k_copy(s).wait()
         scores = []
         top = jnp.full((group, LANES), LOW, jnp.float32)
         for c in range(0, cols, chunk):
@@ -129,7 +139,6 @@
         top_wide = jnp.concatenate([top] * (chunk // LANES), axis=1)
         total = jnp.zeros((group, LANES), jnp.float32)
         part = jnp.zeros((heads, hd), jnp.float32)
-        v_copy(s).wait()
         for i, c in enumerate(range(0, cols, chunk)):
             weight = jnp.where(wide < limit - c, jnp.exp(scores[i] - top_wide), 0.0)
             weight = weight.astype(jnp.bfloat16).astype(jnp.float32)
@@ -146,7 +155,7 @@
         totals[s] = fold(total, kv, jnp.add)
         return carry
 
-    lax.fori_loop(0, slots, one_slot, 0)
+    lax.fori_loop(0, slots, one_slot, 0, unroll=4)
 
     seqs = [slot_block[s] // (slots * n // batch) for s in range(slots)]
     for s in range(slots):
@@ -228,14 +237,16 @@
     f32, bf16 = jnp.float32, jnp.bfloat16
     dma = pltpu.SemaphoreType.DMA
     vmem = pl.BlockSpec(memory_space=pltpu.VMEM)
-    smem = pl.BlockSpec(memory_space=pltpu.SMEM)
-    hbm = pl.BlockSpec(memory_space=pl.ANY)
+    hbm = pl.BlockSpec(memory_space=pltpu.HBM)
     result = pl.pallas_call(
         functools.partial(kernel, n, batch, block, kv, hd ** (-0.5)),
         out_shape=jax.ShapeDtypeStruct((share, hd), bf16),
-        in_specs=[smem, smem, vmem, hbm, hbm],
+        in_specs=[hbm] * 5,
         out_specs=vmem,
         scratch_shapes=[
+            pltpu.SMEM(lengths.shape, jnp.int32),
+            pltpu.SMEM(slot_block.shape, jnp.int32),
+            pltpu.VMEM((share, hd), bf16),
             pltpu.VMEM((n, share, hd), bf16),
             pltpu.VMEM((slots, cols, hd), bf16),
             pltpu.VMEM((slots, cols, hd), bf16),
@@ -250,13 +261,13 @@
             pltpu.VMEM((outer, group, LANES), f32),
             pltpu.VMEM((outer, share, hd), bf16),
             pltpu.VMEM((outer, group, LANES), f32),
-            dma((slots,)), dma((slots,)), dma,
+            dma((slots,)), dma((slots,)), dma, dma((3,)),
             dma((outer,)), dma((n,)), dma((outer,)),
             dma((2,)), dma((2,)),
             dma((outer,)), dma((outer,)), dma((outer,)), dma((outer,)),
         ],
         compiler_params=pltpu.CompilerParams(
-            collective_id=0, has_side_effects=True, vmem_limit_bytes=48 * 1024 * 1024
+            collective_id=0, has_side_effects=True, vmem_limit_bytes=67043328
         ),
         name="decode",
     )(

time: 33.3 us -> 30.7 us (0.922)
  local copies, waits for them, and re-layouts: 2.63 us -> 1.32 us
  Pallas kernels: 30.4 us -> 29.1 us
    pallas_call x1, Pallas kernels: 30.4 us -> 29.1 us  [body(): pl.pallas_call(functools.partial(kernel, n, batch, block, kv, hd ** (-0.5...]
    unnamed x7 -> x1, local copies, waits for them, and re-layouts: 2.63 us -> 1.32 us
where the time goes in v2:
time: 30.7 us; the launch traced here: 30.4 us
  Pallas kernels  29.1 us (95%)
  local copies, waits for them, and re-layouts  1.32 us (4%)
    pallas_call x1, Pallas kernels, body(): pl.pallas_call(functools.partial(kernel, n, batch, block, kv, hd ** (-0.5...  29.1 us
    unnamed x1, local copies, waits for them, and re-layouts  1.32 us

profile of v2, /device:TPU:0, one launch (start us, length us, event | category | flops | bytes accessed | tf_op | source)
XLA Modules:
  0.0 30.4 jit_solution(16368293475047405843)
XLA Ops:
  0.0 29.1 %decode.1 = bf16[64,128]{1,0:T(8,128)(2,1)} custom-call(s32[16]{0:T(128)} %lengths_hbm.1, s32[8]{0:T(128)} %block_hbm.1, bf16[64,128]{1,0:T(8,128)(2,1)} %bitcast.7, bf16[8,4096,128]{2,1,0:T(8,128)(2,1)} %bitcast.4, bf16[8,4096,128]{2,1,0:T(8,128)(2,1)} %bitcast.5), custom_call_target="tpu_custom_call" | custom-call | tf_op jit(solution)/shard_map/decode/pallas_call | solution.py:241
  29.1 1.3 %copy.7 = bf16[64,1,128]{2,0,1:T(8,128)(2,1)} copy(bf16[64,1,128]{2,0,1:T(8,128)(2,1)} %bitcast.6) | data formatting | bytes 32768
